TPU v7x, 32 devices: a whole 2x2x4 slice. The times are simulated.
32 devices in a mesh: section: 2 (over core), rows: 16 (over z, y, x).
Axes of the slice: x: 2, y: 2, z: 4, core: 2. Of those that a mesh axis runs over, the one named last changes fastest.
Arguments:
- table: float32 [16384, 64], P('rows', 'section'), may hold values from -6 to 6
- mask: int32 [16384], P('rows'), may hold values from 0 to 1, as said below
- weight: float32 [64, 1024], replicated, may hold values from -0.75 to 0.75
- bias: float32 [1024], replicated, may hold values from -3 to 3
Outputs:
- projected: bfloat16 [16384, 1024], P('rows', 'section')
Inputs may be any that keep to these rules, and one draw needn't show every extreme that they name: `mask`: the probability that a row survives is constant within one device's rows and drawn afresh for each device, from about 5 to 95 percent.
All inputs are finite; a program needn't handle non-finite values.
Results may differ from a plain program's by a relative error of at most 0.001.
Values sent between devices are 32-bit elements; how exact they have to be, the bound alone decides.
A program may use at most 64 MiB of HBM per device.

v0:
```python
import functools

import jax
import jax.numpy as jnp
from jax import lax
from jax.experimental import pallas as pl
from jax.experimental.pallas import tpu as pltpu
from jax.sharding import PartitionSpec as P

CHUNKS = 4
PLANE = 4
RAW = 4
F32 = jnp.float32
BF16 = jnp.bfloat16
I32 = jnp.int32


def split(x, terms):
    parts = []
    for _ in range(terms):
        part = x.astype(BF16)
        parts.append(part)
        x = x - part.astype(F32)
    return parts


def kernel(
    n, table_hbm, mask_hbm, w_hbm, bias_hbm, out_ref,
    table_ref, mask_ref, bias_ref,
    tally, planes, prefix, raw, hold, came, joined, w_ref, wcat,
    send_sem, recv_sem, raw_send, raw_recv, count_send, count_recv, plane_send, plane_recv, load_sem,
):
    half, height = table_hbm.shape
    width = out_ref.shape[1]
    lines = height // 128
    levels = (n - 1).bit_length()
    lanes = height // CHUNKS
    side = min(PLANE, n)
    crowd = min(RAW, n)
    first = (crowd - 1).bit_length()
    count_planes = n // side
    me = lax.axis_index("rows")
    core = lax.axis_index("section")
    plane = me // side
    seat = lax.rem(me, side)

    columns = pl.ds(pl.multiple_of(core * width, 128), width)
    mask_copy = pltpu.make_async_copy(mask_hbm, mask_ref, load_sem.at[0])
    table_copy = pltpu.make_async_copy(table_hbm, table_ref, load_sem.at[1])
    w_copy = pltpu.make_async_copy(w_hbm.at[:, columns], w_ref, load_sem.at[2])
    bias_copy = pltpu.make_async_copy(bias_hbm.at[:, columns], bias_ref, load_sem.at[3])
    for load in (mask_copy, table_copy, w_copy, bias_copy):
        load.start()

    def seat_peer(step):
        return plane * side + lax.rem(seat + step, side)

    def plane_peer(step):
        return lax.rem(plane + step, count_planes) * side + seat

    barrier = pltpu.get_barrier_semaphore()
    for step in range(1, side):
        pl.semaphore_signal(barrier, inc=1, device_id={"rows": seat_peer(step)})
    for step in range(1, count_planes):
        pl.semaphore_signal(barrier, inc=1, device_id={"rows": plane_peer(step)})
    pl.semaphore_signal(barrier, inc=1, device_id={"section": 1 - core})

    mask_copy.wait()
    mask = mask_ref[...]
    ones = mask.astype(F32).astype(BF16)
    row = lax.broadcasted_iota(I32, (128, 128), 0)
    col = lax.broadcasted_iota(I32, (128, 128), 1)
    before = jnp.where(row < col, 1.0, 0.0).astype(BF16)
    inner = jnp.dot(ones, before, preferred_element_type=F32).astype(I32)
    sums = jnp.dot(ones, jnp.ones((128, 128), BF16), preferred_element_type=F32).astype(I32)
    running = jnp.zeros((1, 128), I32)
    starts = []
    for line in range(lines):
        starts.append(running)
        running = running + sums[line : line + 1]
    tally[seat] = running
    slot = jnp.where(mask == 1, inner + jnp.concatenate(starts, 0), -1)

    own = lax.rem(me, crowd)
    table_copy.wait()
    turned = jnp.concatenate(split(table_ref[...], 3), 0)
    for chunk in range(CHUNKS):
        here = chunk * lanes + lax.broadcasted_iota(I32, (lanes, 128), 0)
        hot = jnp.concatenate(
            [jnp.where(here == slot[b : b + 1], 1.0, 0.0).astype(BF16) for b in range(chunk * lanes // 128, lines)], 1
        )
        folded = lax.dot_general(
            turned[:, chunk * lanes :], hot, (((1,), (1,)), ((), ())), preferred_element_type=F32
        )
        raw[own, :, chunk * lanes : (chunk + 1) * lanes] = (
            folded[:half] + folded[half : 2 * half]
        ) + folded[2 * half :]

    pl.semaphore_wait(barrier, side + count_planes - 1)

    def seat_copy(step):
        return pltpu.make_async_remote_copy(
            src_ref=tally.at[seat], dst_ref=tally.at[seat],
            send_sem=count_send.at[step], recv_sem=count_recv.at[step],
            device_id={"rows": seat_peer(step)},
        )

    def plane_copy(step):
        return pltpu.make_async_remote_copy(
            src_ref=planes.at[plane], dst_ref=planes.at[plane],
            send_sem=plane_send.at[step], recv_sem=plane_recv.at[step],
            device_id={"rows": plane_peer(step)},
        )

    def raw_copy(step):
        return pltpu.make_async_remote_copy(
            src_ref=raw.at[own], dst_ref=raw.at[own],
            send_sem=raw_send.at[step], recv_sem=raw_recv.at[step],
            device_id={"rows": me - own + lax.rem(own + step, crowd)},
        )

    for step in range(1, side):
        seat_copy(step).start()
    for step in range(1, crowd):
        raw_copy(step).start()
    for step in range(1, side):
        seat_copy(step).wait_recv()
    everyone = jnp.zeros((1, 128), I32)
    for at in range(side):
        everyone = everyone + tally[at]
    planes[plane] = everyone
    for step in range(1, count_planes):
        plane_copy(step).start()

    w_copy.wait()
    bias_copy.wait()
    bias = bias_ref[...]
    w_hi, w_lo = split(w_ref[...], 2)
    b_hi, b_mid, b_lo = [part.astype(F32) for part in split(bias, 3)]
    line = lax.broadcasted_iota(I32, (16, width), 0)
    extra = jnp.where(line == 0, b_hi, jnp.where(line == 1, b_mid, jnp.where(line == 2, b_lo, 0.0)))
    wcat[...] = jnp.concatenate([w_hi, w_lo, w_hi, extra.astype(BF16)], 0)

    for step in range(1, count_planes):
        plane_copy(step).wait_recv()
    total = jnp.zeros((1, 128), I32)
    for at in range(count_planes):
        prefix[at * side] = total
        total = total + planes[at]
    prefix[n] = total
    running = prefix[plane * side]
    for at in range(side - 1):
        running = running + tally[at]
        prefix[plane * side + at + 1] = running

    def wide(x):
        return jnp.concatenate([x] * (lanes // 128), 1)

    def data_copy(level, chunk):
        at = (slice(None), pl.ds(chunk * lanes, lanes))
        return pltpu.make_async_remote_copy(
            src_ref=hold.at[(level,) + at], dst_ref=came.at[(level,) + at],
            send_sem=send_sem.at[level, chunk], recv_sem=recv_sem.at[level, chunk],
            device_id={"rows": me + (1 - 2 * (me // (1 << level) % 2)) * (1 << level)},
        )

    def join_copy(chunk):
        at = (core, slice(None), pl.ds(chunk * lanes, lanes))
        return pltpu.make_async_remote_copy(
            src_ref=joined.at[at], dst_ref=joined.at[at],
            send_sem=send_sem.at[levels, chunk], recv_sem=recv_sem.at[levels, chunk],
            device_id={"section": 1 - core},
        )

    for step in range(1, crowd):
        raw_copy(step).wait_recv()
    turns = []
    for at in range(crowd):
        shift = (prefix[me - own + at] & (height - 1))[0, 0]
        turns.append(pltpu.roll(raw[at], shift, 1))
    low = wide(prefix[me - own])
    for chunk in range(CHUNKS):
        at = slice(chunk * lanes, (chunk + 1) * lanes)
        base = own * height + chunk * lanes + lax.broadcasted_iota(I32, (1, lanes), 1)
        place = low + ((base - low) & (crowd * height - 1))
        place = jnp.broadcast_to(place, (half, lanes))
        block = turns[0][:, at]
        for other in range(1, crowd):
            block = jnp.where(place >= wide(prefix[me - own + other]), turns[other][:, at], block)
        hold[first, :, at] = block
        data_copy(first, chunk).start()

    for level in range(first, levels):
        reach = 2 << level
        group = me // reach * reach
        bit = me // (1 << level) % 2
        low = wide(prefix[group])
        middle = wide(prefix[group + (1 << level)])
        for chunk in range(CHUNKS):
            at = slice(chunk * lanes, (chunk + 1) * lanes)
            data_copy(level, chunk).wait_recv()
            base = (me % reach) * height + chunk * lanes
            base = base + lax.broadcasted_iota(I32, (1, lanes), 1)
            place = low + ((base - low) & (reach * height - 1))
            upper = jnp.where(place >= middle, 1, 0)
            foreign = jnp.broadcast_to(upper, (half, lanes)) != bit
            block = jnp.where(foreign, came[level, :, at], hold[level, :, at])
            if level < levels - 1:
                hold[level + 1, :, at] = block
                data_copy(level + 1, chunk).start()
            else:
                joined[core, :, at] = block
                join_copy(chunk).start()

    ends = wide(total)
    for chunk in range(CHUNKS):
        at = slice(chunk * lanes, (chunk + 1) * lanes)
        join_copy(chunk).wait_recv()
        owned = me * height + chunk * lanes + lax.broadcasted_iota(I32, (1, lanes), 1)
        filled = jnp.where(owned < ends, 1.0, 0.0)
        rows = jnp.concatenate([joined[0, :, at], joined[1, :, at]], 0)
        rows = jnp.where(jnp.broadcast_to(filled, rows.shape) > 0.5, rows, 0.0)
        a_hi, a_lo = split(rows, 2)
        marks = jnp.broadcast_to(filled, (16, lanes)).astype(BF16)
        lhs = jnp.concatenate([a_hi, a_hi, a_lo, marks], 0)
        out_ref[at, :] = lax.dot_general(
            lhs, wcat[...], (((0,), (0,)), ((), ())), preferred_element_type=F32
        ).astype(BF16)

    for step in range(1, side):
        seat_copy(step).wait_send()
    for step in range(1, count_planes):
        plane_copy(step).wait_send()
    for step in range(1, crowd):
        raw_copy(step).wait_send()
    for level in range(first, levels):
        for chunk in range(CHUNKS):
            data_copy(level, chunk).wait_send()
    for chunk in range(CHUNKS):
        join_copy(chunk).wait_send()


def solution(mesh):
    n, sections = mesh.shape["rows"], mesh.shape["section"]

    def step(table, mask, weight, bias):
        height, half = table.shape
        cols, features = weight.shape
        width = features // sections
        levels = (n - 1).bit_length()
        side, crowd = min(PLANE, n), min(RAW, n)
        operands = table.T, mask.reshape(height // 128, 128), weight, bias.reshape(1, features)
        vmem = pl.BlockSpec(memory_space=pltpu.VMEM)
        sem = pltpu.SemaphoreType.DMA
        return pl.pallas_call(
            functools.partial(kernel, n),
            name="filter_project",
            out_shape=jax.ShapeDtypeStruct((height, width), BF16),
            in_specs=[pl.BlockSpec(memory_space=pltpu.HBM)] * 4,
            out_specs=vmem,
            scratch_shapes=[
                pltpu.VMEM((half, height), F32),
                pltpu.VMEM((height // 128, 128), I32),
                pltpu.VMEM((1, width), F32),
                pltpu.VMEM((side, 1, 128), I32),
                pltpu.VMEM((n // side, 1, 128), I32),
                pltpu.VMEM((n + 1, 1, 128), I32),
                pltpu.VMEM((crowd, half, height), F32),
                pltpu.VMEM((levels, half, height), F32),
                pltpu.VMEM((levels, half, height), F32),
                pltpu.VMEM((sections, half, height), F32),
                pltpu.VMEM((cols, width), F32),
                pltpu.VMEM((3 * cols + 16, width), BF16),
                sem((levels + 1, CHUNKS)), sem((levels + 1, CHUNKS)),
                sem((crowd,)), sem((crowd,)),
                sem((side,)), sem((side,)),
                sem((n // side,)), sem((n // side,)),
                sem((4,)),
            ],
            compiler_params=pltpu.CompilerParams(
                collective_id=0, has_side_effects=True, vmem_limit_bytes=16 << 20
            ),
        )(*[pltpu.with_memory_space_constraint(x, pltpu.HBM) for x in operands])

    return jax.shard_map(
        step,
        mesh=mesh,
        in_specs=(P("rows", "section"), P("rows"), P(), P()),
        out_specs=P("rows", "section"),
        check_vma=False,
    )
```

profile of v0, /device:TPU:0, one launch (start us, length us, event | category | flops | bytes accessed | tf_op | source)
XLA Modules:
  0.0 25.0 jit_solution(12064830996008831662)
XLA Ops:
  0.0 24.0 %filter_project.1 = bf16[1024,512]{1,0:T(8,128)(2,1)S(1)} custom-call(f32[32,1024]{1,0:T(8,128)} %bitcast.3, s32[8,128]{1,0:T(8,128)} %bitcast.4, f32[64,1024]{1,0:T(8,128)} %w_hbm.1, f32[1,1024]{1,0:T(1,128)} %bitcast.5), custom_call_target="tpu_custom_call" | custom-call | tf_op jit(solution)/shard_map/filter_project/pallas_call | solution.py:255
  24.0 1.0 %copy.6 = bf16[1024,512]{1,0:T(8,128)(2,1)} copy(bf16[1024,512]{1,0:T(8,128)(2,1)S(1)} %filter_project.1) | data formatting | bytes 2097152
where the time goes:
time: 25.1 us; the launch traced here: 25 us
  Pallas kernels  24 us (96%)
  local copies, waits for them, and re-layouts  0.97 us (4%)
    pallas_call x1, Pallas kernels, step(): pl.pallas_call(functools.partial(kernel, n), name='filter_project', out_s...  24 us
    unnamed x1, local copies, waits for them, and re-layouts  0.97 us

commit v1 on v0

--- a/solution.py
+++ b/solution.py
@@ -10,6 +10,9 @@
 CHUNKS = 4
 PLANE = 4
 RAW = 4
+LINES = 4
+GROUP = 8
+TERMS = 2
 F32 = jnp.float32
 BF16 = jnp.bfloat16
 I32 = jnp.int32
@@ -24,7 +27,7 @@
     return parts
 
 
-def kernel(
+def butterfly(
     n, table_hbm, mask_hbm, w_hbm, bias_hbm, out_ref,
     table_ref, mask_ref, bias_ref,
     tally, planes, prefix, raw, hold, came, joined, w_ref, wcat,
@@ -240,6 +243,303 @@
         join_copy(chunk).wait_send()
 
 
+def wide(x, lanes):
+    return jnp.concatenate([x] * (lanes // 128), 1)
+
+
+def flip(at, step, extent):
+    out, bit = 0, 1
+    while bit < extent:
+        a, b = at // bit % 2, step // bit % 2
+        out = out + bit * (a + b - 2 * a * b)
+        bit *= 2
+    return out
+
+
+def direct(
+    n, table_hbm, mask_hbm, w_hbm, bias_hbm, out_ref,
+    table_ref, mask_ref, bias_ref,
+    tally, prefix, gather, turned, pieces, got, joined, w_ref, wcat,
+    load_sem, count_send, count_recv, gather_send, gather_recv, relay_send,
+    piece_send, piece_recv, join_send, join_recv,
+):
+    half, height = table_hbm.shape
+    width = out_ref.shape[1]
+    rows = height // 128
+    lanes = height // CHUNKS
+    groups = half // GROUP
+    side = min(PLANE, n)
+    lines = n // side
+    me = lax.axis_index("rows")
+    core = lax.axis_index("section")
+    line = me // side
+    seat = lax.rem(me, side)
+    flat = core == 1
+
+    columns = pl.ds(pl.multiple_of(core * width, 128), width)
+    mask_copy = pltpu.make_async_copy(mask_hbm, mask_ref, load_sem.at[0])
+    table_copy = pltpu.make_async_copy(table_hbm, table_ref, load_sem.at[1])
+    w_copy = pltpu.make_async_copy(w_hbm.at[:, columns], w_ref, load_sem.at[2])
+    bias_copy = pltpu.make_async_copy(bias_hbm.at[:, columns], bias_ref, load_sem.at[3])
+    for load in (mask_copy, table_copy, w_copy, bias_copy):
+        load.start()
+
+    barrier = pltpu.get_barrier_semaphore()
+    for step in range(1, n):
+        pl.semaphore_signal(barrier, inc=1, device_id={"rows": lax.rem(me + step, n)})
+    pl.semaphore_signal(barrier, inc=1, device_id={"section": 1 - core})
+
+    mask_copy.wait()
+    mask = mask_ref[...]
+    ones = mask.astype(F32).astype(BF16)
+    row = lax.broadcasted_iota(I32, (128, 128), 0)
+    col = lax.broadcasted_iota(I32, (128, 128), 1)
+    before = jnp.where(row < col, 1.0, 0.0).astype(BF16)
+    inner = jnp.dot(ones, before, preferred_element_type=F32).astype(I32)
+    sums = jnp.dot(ones, jnp.ones((128, 128), BF16), preferred_element_type=F32).astype(I32)
+    running = jnp.zeros((1, 128), I32)
+    starts = []
+    for at in range(rows):
+        starts.append(running)
+        running = running + sums[at : at + 1]
+    tally[me] = running
+    slot = jnp.where(mask == 1, inner + jnp.concatenate(starts, 0), -1)
+
+    own = jnp.where(flat, seat, line)
+    table_copy.wait()
+    terms = jnp.concatenate(split(table_ref[...], TERMS), 0)
+    for chunk in range(CHUNKS):
+        here = chunk * lanes + lax.broadcasted_iota(I32, (lanes, 128), 0)
+        hot = jnp.concatenate(
+            [jnp.where(here == slot[b : b + 1], 1.0, 0.0).astype(BF16) for b in range(chunk * lanes // 128, rows)], 1
+        )
+        folded = lax.dot_general(
+            terms[:, chunk * lanes :], hot, (((1,), (1,)), ((), ())), preferred_element_type=F32
+        )
+        total = folded[:half]
+        for term in range(1, TERMS):
+            total = total + folded[term * half : (term + 1) * half]
+        gather[own, :, chunk * lanes : (chunk + 1) * lanes] = total
+
+    pl.semaphore_wait(barrier, n)
+
+    def count_copy(step):
+        return pltpu.make_async_remote_copy(
+            src_ref=tally.at[me], dst_ref=tally.at[me],
+            send_sem=count_send.at[step], recv_sem=count_recv.at[step],
+            device_id={"rows": lax.rem(me + step, n)},
+        )
+
+    def seat_copy(step, g):
+        at = (seat, pl.ds(g * GROUP, GROUP))
+        return pltpu.make_async_remote_copy(
+            src_ref=gather.at[at], dst_ref=gather.at[at],
+            send_sem=gather_send.at[step, g], recv_sem=gather_recv.at[step, g],
+            device_id={"rows": line * side + flip(seat, step, side)},
+        )
+
+    def line_copy(source, target, g):
+        at = (source, pl.ds(g * GROUP, GROUP))
+        return pltpu.make_async_remote_copy(
+            src_ref=gather.at[at], dst_ref=gather.at[at],
+            send_sem=gather_send.at[target, g], recv_sem=gather_recv.at[source, g],
+            device_id={"rows": target * side + seat},
+        )
+
+    def relay_copy(source, g):
+        at = (source, pl.ds(g * GROUP, GROUP))
+        return pltpu.make_async_remote_copy(
+            src_ref=gather.at[at], dst_ref=gather.at[at],
+            send_sem=relay_send.at[source, g], recv_sem=gather_recv.at[source, g],
+            device_id={"rows": side + seat},
+        )
+
+    def down_copy(source, target, g):
+        at = pl.ds(g * GROUP, GROUP)
+        return pltpu.make_async_remote_copy(
+            src_ref=pieces.at[target, at], dst_ref=got.at[source, at],
+            send_sem=piece_send.at[target, g], recv_sem=piece_recv.at[source, g],
+            device_id={"rows": target * side + seat},
+        )
+
+    def across_copy(step, g):
+        at = pl.ds(g * GROUP, GROUP)
+        return pltpu.make_async_remote_copy(
+            src_ref=pieces.at[step, at], dst_ref=got.at[step, at],
+            send_sem=piece_send.at[step, g], recv_sem=piece_recv.at[step, g],
+            device_id={"rows": line * side + flip(seat, step, side)},
+        )
+
+    def join_copy(g):
+        at = (core, pl.ds(g * GROUP, GROUP))
+        return pltpu.make_async_remote_copy(
+            src_ref=joined.at[at], dst_ref=joined.at[at],
+            send_sem=join_send.at[g], recv_sem=join_recv.at[g],
+            device_id={"section": 1 - core},
+        )
+
+    for step in range(1, n):
+        count_copy(step).start()
+
+    @pl.when(flat)
+    def _():
+        for g in range(groups):
+            for step in range(1, side):
+                seat_copy(step, g).start()
+
+    for source in range(1, lines):
+        @pl.when(jnp.logical_and(core == 0, line == source))
+        def _(source=source):
+            for target in range(source):
+                if target != 1:
+                    for g in range(groups):
+                        line_copy(source, target, g).start()
+
+    w_copy.wait()
+    bias_copy.wait()
+    bias = bias_ref[...]
+    w_hi, w_lo = split(w_ref[...], 2)
+    b_hi, b_mid, b_lo = [part.astype(F32) for part in split(bias, 3)]
+    at = lax.broadcasted_iota(I32, (16, width), 0)
+    extra = jnp.where(at == 0, b_hi, jnp.where(at == 1, b_mid, jnp.where(at == 2, b_lo, 0.0)))
+    wcat[...] = jnp.concatenate([w_hi, w_lo, w_hi, extra.astype(BF16)], 0)
+
+    for step in range(1, n):
+        count_copy(step).wait_recv()
+    total = jnp.zeros((1, 128), I32)
+    for at in range(n):
+        prefix[at] = total
+        total = total + tally[at]
+    prefix[n] = total
+
+    lane = lax.broadcasted_iota(I32, (GROUP, height), 1)
+
+    def bound(index):
+        return wide(jnp.broadcast_to(prefix[index], (GROUP, 128)), height)
+
+    def turn(slot, index, g):
+        shift = (prefix[index] & (height - 1))[0, 0]
+        return pltpu.roll(gather[slot, g * GROUP : (g + 1) * GROUP], shift, 1)
+
+    @pl.when(flat)
+    def _():
+        for g in range(groups):
+            rows_g = slice(g * GROUP, (g + 1) * GROUP)
+            for step in range(1, side):
+                seat_copy(step, g).wait_recv()
+            blocks = [turn(at, line * side + at, g) for at in range(side)]
+            for target in range(lines):
+                place = (target * side + seat) * height + lane
+                piece = jnp.where(place >= bound(line * side), blocks[0], 0.0)
+                for at in range(1, side):
+                    piece = jnp.where(place >= bound(line * side + at), blocks[at], piece)
+                pieces[target, rows_g] = jnp.where(place >= bound(line * side + side), 0.0, piece)
+                if target == 0:
+                    @pl.when(line > 0)
+                    def _(g=g):
+                        for source in range(1, lines):
+                            @pl.when(line == source)
+                            def _(source=source):
+                                down_copy(source, 0, g).start()
+        for source in range(2, lines):
+            @pl.when(line == source)
+            def _(source=source):
+                for target in range(1, source):
+                    for g in range(groups):
+                        down_copy(source, target, g).start()
+
+        for g in range(groups):
+            rows_g = slice(g * GROUP, (g + 1) * GROUP)
+            joined[1, rows_g] = pieces[line, rows_g]
+            for source in range(1, lines):
+                @pl.when(line < source)
+                def _(source=source, g=g, rows_g=rows_g):
+                    down_copy(source, line, g).wait_recv()
+                    joined[1, rows_g] = joined[1, rows_g] + got[source, rows_g]
+            join_copy(g).start()
+
+    @pl.when(core == 0)
+    def _():
+        for g in range(groups):
+            rows_g = slice(g * GROUP, (g + 1) * GROUP)
+            for source in range(1, lines):
+                @pl.when(line < source)
+                def _(source=source, g=g):
+                    line_copy(source, line, g).wait_recv()
+                if source >= 2:
+                    @pl.when(line == 0)
+                    def _(source=source, g=g):
+                        relay_copy(source, g).start()
+            blocks = [turn(at, at * side + seat, g) for at in range(lines)]
+            for step in list(range(1, side)) + [0]:
+                place = (line * side + flip(seat, step, side)) * height + lane
+                piece = jnp.zeros((GROUP, height), F32)
+                for at in range(lines):
+                    index = at * side + seat
+                    inside = jnp.logical_and(place >= bound(index), place < bound(index + 1))
+                    piece = jnp.where(inside, blocks[at], piece)
+                pieces[step, rows_g] = piece
+                if step:
+                    across_copy(step, g).start()
+        for g in range(groups):
+            rows_g = slice(g * GROUP, (g + 1) * GROUP)
+            total = pieces[0, rows_g]
+            for step in range(1, side):
+                across_copy(step, g).wait_recv()
+                total = total + got[step, rows_g]
+            joined[0, rows_g] = total
+            join_copy(g).start()
+
+    for g in range(groups):
+        join_copy(g).wait_recv()
+    ends = wide(prefix[n], lanes)
+    for chunk in range(CHUNKS):
+        at = slice(chunk * lanes, (chunk + 1) * lanes)
+        owned = me * height + chunk * lanes + lax.broadcasted_iota(I32, (1, lanes), 1)
+        filled = jnp.where(owned < ends, 1.0, 0.0)
+        block = jnp.concatenate([joined[0, :, at], joined[1, :, at]], 0)
+        a_hi, a_lo = split(block, 2)
+        marks = jnp.broadcast_to(filled, (16, lanes)).astype(BF16)
+        lhs = jnp.concatenate([a_hi, a_hi, a_lo, marks], 0)
+        out_ref[at, :] = lax.dot_general(
+            lhs, wcat[...], (((0,), (0,)), ((), ())), preferred_element_type=F32
+        ).astype(BF16)
+
+    for step in range(1, n):
+        count_copy(step).wait_send()
+    for g in range(groups):
+        join_copy(g).wait_send()
+
+    @pl.when(flat)
+    def _():
+        for g in range(groups):
+            for step in range(1, side):
+                seat_copy(step, g).wait_send()
+        for source in range(1, lines):
+            @pl.when(line == source)
+            def _(source=source):
+                for target in range(source):
+                    for g in range(groups):
+                        down_copy(source, target, g).wait_send()
+
+    @pl.when(core == 0)
+    def _():
+        for source in range(1, lines):
+            @pl.when(line == source)
+            def _(source=source):
+                for target in range(source):
+                    if target != 1:
+                        for g in range(groups):
+                            line_copy(source, target, g).wait_send()
+        for g in range(groups):
+            for source in range(2, lines):
+                @pl.when(line == 0)
+                def _(source=source, g=g):
+                    relay_copy(source, g).wait_send()
+            for step in range(1, side):
+                across_copy(step, g).wait_send()
+
+
 def solution(mesh):
     n, sections = mesh.shape["rows"], mesh.shape["section"]
 
@@ -249,19 +549,37 @@
         width = features // sections
         levels = (n - 1).bit_length()
         side, crowd = min(PLANE, n), min(RAW, n)
+        lines, groups = n // side, half // GROUP
         operands = table.T, mask.reshape(height // 128, 128), weight, bias.reshape(1, features)
-        vmem = pl.BlockSpec(memory_space=pltpu.VMEM)
         sem = pltpu.SemaphoreType.DMA
-        return pl.pallas_call(
-            functools.partial(kernel, n),
-            name="filter_project",
-            out_shape=jax.ShapeDtypeStruct((height, width), BF16),
-            in_specs=[pl.BlockSpec(memory_space=pltpu.HBM)] * 4,
-            out_specs=vmem,
-            scratch_shapes=[
-                pltpu.VMEM((half, height), F32),
-                pltpu.VMEM((height // 128, 128), I32),
-                pltpu.VMEM((1, width), F32),
+        loads = [
+            pltpu.VMEM((half, height), F32),
+            pltpu.VMEM((height // 128, 128), I32),
+            pltpu.VMEM((1, width), F32),
+        ]
+        weights = [
+            pltpu.VMEM((cols, width), F32),
+            pltpu.VMEM((3 * cols + 16, width), BF16),
+        ]
+        if lines <= LINES:
+            most = max(side, lines)
+            block = pltpu.VMEM((most, half, height), F32)
+            body = direct
+            scratch = loads + [
+                pltpu.VMEM((n, 1, 128), I32),
+                pltpu.VMEM((n + 1, 1, 128), I32),
+                block, block, block, block,
+                pltpu.VMEM((sections, half, height), F32),
+            ] + weights + [
+                sem((4,)),
+                sem((n,)), sem((n,)),
+                sem((most, groups)), sem((most, groups)), sem((most, groups)),
+                sem((most, groups)), sem((most, groups)),
+                sem((groups,)), sem((groups,)),
+            ]
+        else:
+            body = butterfly
+            scratch = loads + [
                 pltpu.VMEM((side, 1, 128), I32),
                 pltpu.VMEM((n // side, 1, 128), I32),
                 pltpu.VMEM((n + 1, 1, 128), I32),
@@ -269,14 +587,20 @@
                 pltpu.VMEM((levels, half, height), F32),
                 pltpu.VMEM((levels, half, height), F32),
                 pltpu.VMEM((sections, half, height), F32),
-                pltpu.VMEM((cols, width), F32),
-                pltpu.VMEM((3 * cols + 16, width), BF16),
+            ] + weights + [
                 sem((levels + 1, CHUNKS)), sem((levels + 1, CHUNKS)),
                 sem((crowd,)), sem((crowd,)),
                 sem((side,)), sem((side,)),
                 sem((n // side,)), sem((n // side,)),
                 sem((4,)),
-            ],
+            ]
+        return pl.pallas_call(
+            functools.partial(body, n),
+            name="filter_project",
+            out_shape=jax.ShapeDtypeStruct((height, width), BF16),
+            in_specs=[pl.BlockSpec(memory_space=pltpu.HBM)] * 4,
+            out_specs=pl.BlockSpec(memory_space=pltpu.VMEM),
+            scratch_shapes=scratch,
             compiler_params=pltpu.CompilerParams(
                 collective_id=0, has_side_effects=True, vmem_limit_bytes=16 << 20
             ),

time: 25.1 us -> 25.8 us (1.028)
  the two profiles are of different devices: /device:TPU:0 before, /device:TPU:9 now
where the time goes in v1:
time: 25.8 us; the launch traced here: 25.7 us
  Pallas kernels  24.7 us (96%)
  local copies, waits for them, and re-layouts  0.97 us (4%)
    pallas_call x1, Pallas kernels, step(): pl.pallas_call(functools.partial(body, n), name='filter_project', out_sha...  24.7 us
    unnamed x1, local copies, waits for them, and re-layouts  0.97 us

profile of v1, /device:TPU:9, one launch (start us, length us, event | category | flops | bytes accessed | tf_op | source)
XLA Modules:
  0.0 25.7 jit_solution(1832962427598465477)
XLA Ops:
  0.0 24.7 %filter_project.1 = bf16[1024,512]{1,0:T(8,128)(2,1)S(1)} custom-call(f32[32,1024]{1,0:T(8,128)} %bitcast.3, s32[8,128]{1,0:T(8,128)} %bitcast.4, f32[64,1024]{1,0:T(8,128)} %w_hbm.1, f32[1,1024]{1,0:T(1,128)} %bitcast.5), custom_call_target="tpu_custom_call" | custom-call | tf_op jit(solution)/shard_map/filter_project/pallas_call | solution.py:597
  24.7 1.0 %copy.6 = bf16[1024,512]{1,0:T(8,128)(2,1)} copy(bf16[1024,512]{1,0:T(8,128)(2,1)S(1)} %filter_project.1) | data formatting | bytes 2097152

commit v2 on v1

--- a/solution.py
+++ b/solution.py
@@ -259,9 +259,9 @@
 def direct(
     n, table_hbm, mask_hbm, w_hbm, bias_hbm, out_ref,
     table_ref, mask_ref, bias_ref,
-    tally, prefix, gather, turned, pieces, got, joined, w_ref, wcat,
-    load_sem, count_send, count_recv, gather_send, gather_recv, relay_send,
-    piece_send, piece_recv, join_send, join_recv,
+    tally, prefix, gather, pieces, got, joined, w_ref, wcat,
+    load_sem, count_send, count_recv, gather_send, gather_recv,
+    piece_send, piece_recv, across_send, across_recv, join_send, join_recv,
 ):
     half, height = table_hbm.shape
     width = out_ref.shape[1]
@@ -285,9 +285,21 @@
         load.start()
 
     barrier = pltpu.get_barrier_semaphore()
-    for step in range(1, n):
-        pl.semaphore_signal(barrier, inc=1, device_id={"rows": lax.rem(me + step, n)})
     pl.semaphore_signal(barrier, inc=1, device_id={"section": 1 - core})
+
+    @pl.when(flat)
+    def _():
+        for step in range(1, n):
+            pl.semaphore_signal(barrier, inc=1, device_id={"rows": lax.rem(me + step, n)})
+
+    @pl.when(core == 0)
+    def _():
+        for step in range(1, side):
+            pl.semaphore_signal(barrier, inc=1, device_id={"rows": line * side + flip(seat, step, side)})
+        for other in range(1, lines):
+            @pl.when(line < other)
+            def _(other=other):
+                pl.semaphore_signal(barrier, inc=1, device_id={"rows": other * side + seat})
 
     mask_copy.wait()
     mask = mask_ref[...]
@@ -316,73 +328,66 @@
         folded = lax.dot_general(
             terms[:, chunk * lanes :], hot, (((1,), (1,)), ((), ())), preferred_element_type=F32
         )
-        total = folded[:half]
+        block = folded[:half]
         for term in range(1, TERMS):
-            total = total + folded[term * half : (term + 1) * half]
-        gather[own, :, chunk * lanes : (chunk + 1) * lanes] = total
-
-    pl.semaphore_wait(barrier, n)
+            block = block + folded[term * half : (term + 1) * half]
+        gather[own, :, chunk * lanes : (chunk + 1) * lanes] = block
+
+    def span(g):
+        return pl.ds(g * GROUP, GROUP)
+
+    def remote(src, dst, send, recv, **to):
+        return pltpu.make_async_remote_copy(src_ref=src, dst_ref=dst, send_sem=send, recv_sem=recv, device_id=to)
+
+    def blocks_of(count, g):
+        return gather.at[pl.ds(0, count), span(g)]
 
     def count_copy(step):
-        return pltpu.make_async_remote_copy(
-            src_ref=tally.at[me], dst_ref=tally.at[me],
-            send_sem=count_send.at[step], recv_sem=count_recv.at[step],
-            device_id={"rows": lax.rem(me + step, n)},
-        )
+        return remote(tally.at[me], tally.at[me], count_send.at[0], count_recv.at[0], rows=lax.rem(me + step, n))
+
+    def prefix_copy():
+        return remote(prefix, prefix, count_send.at[1], count_recv.at[1], section=1 - core)
 
     def seat_copy(step, g):
-        at = (seat, pl.ds(g * GROUP, GROUP))
-        return pltpu.make_async_remote_copy(
-            src_ref=gather.at[at], dst_ref=gather.at[at],
-            send_sem=gather_send.at[step, g], recv_sem=gather_recv.at[step, g],
-            device_id={"rows": line * side + flip(seat, step, side)},
-        )
+        at = gather.at[seat, span(g)]
+        to = line * side + flip(seat, step, side)
+        return remote(at, at, gather_send.at[0], gather_recv.at[g], rows=to)
 
     def line_copy(source, target, g):
-        at = (source, pl.ds(g * GROUP, GROUP))
-        return pltpu.make_async_remote_copy(
-            src_ref=gather.at[at], dst_ref=gather.at[at],
-            send_sem=gather_send.at[target, g], recv_sem=gather_recv.at[source, g],
-            device_id={"rows": target * side + seat},
-        )
-
-    def relay_copy(source, g):
-        at = (source, pl.ds(g * GROUP, GROUP))
-        return pltpu.make_async_remote_copy(
-            src_ref=gather.at[at], dst_ref=gather.at[at],
-            send_sem=relay_send.at[source, g], recv_sem=gather_recv.at[source, g],
-            device_id={"rows": side + seat},
-        )
+        at = gather.at[source, span(g)]
+        return remote(at, at, gather_send.at[0], gather_recv.at[g], rows=target * side + seat)
 
     def down_copy(source, target, g):
-        at = pl.ds(g * GROUP, GROUP)
-        return pltpu.make_async_remote_copy(
-            src_ref=pieces.at[target, at], dst_ref=got.at[source, at],
-            send_sem=piece_send.at[target, g], recv_sem=piece_recv.at[source, g],
-            device_id={"rows": target * side + seat},
+        return remote(
+            pieces.at[target, span(g)], got.at[source, span(g)],
+            piece_send.at[0], piece_recv.at[g], rows=target * side + seat,
         )
 
     def across_copy(step, g):
-        at = pl.ds(g * GROUP, GROUP)
-        return pltpu.make_async_remote_copy(
-            src_ref=pieces.at[step, at], dst_ref=got.at[step, at],
-            send_sem=piece_send.at[step, g], recv_sem=piece_recv.at[step, g],
-            device_id={"rows": line * side + flip(seat, step, side)},
+        return remote(
+            pieces.at[step, span(g)], got.at[step, span(g)],
+            across_send.at[0], across_recv.at[g], rows=line * side + flip(seat, step, side),
         )
 
     def join_copy(g):
-        at = (core, pl.ds(g * GROUP, GROUP))
-        return pltpu.make_async_remote_copy(
-            src_ref=joined.at[at], dst_ref=joined.at[at],
-            send_sem=join_send.at[g], recv_sem=join_recv.at[g],
-            device_id={"section": 1 - core},
-        )
-
-    for step in range(1, n):
-        count_copy(step).start()
+        at = joined.at[core, span(g)]
+        return remote(at, at, join_send.at[0], join_recv.at[0], section=1 - core)
+
+    def arrived(count, g, sem):
+        at = blocks_of(count, g)
+        remote(at, at, sem, sem, section=core).wait_recv()
+
+    def left(count, sem):
+        for at in range(0, count, side):
+            some = gather.at[pl.ds(0, min(side, count - at))]
+            remote(some, some, sem, sem, section=core).wait_send()
+
+    pl.semaphore_wait(barrier, jnp.where(flat, n, side + line))
 
     @pl.when(flat)
     def _():
+        for step in range(1, n):
+            count_copy(step).start()
         for g in range(groups):
             for step in range(1, side):
                 seat_copy(step, g).start()
@@ -391,9 +396,8 @@
         @pl.when(jnp.logical_and(core == 0, line == source))
         def _(source=source):
             for target in range(source):
-                if target != 1:
-                    for g in range(groups):
-                        line_copy(source, target, g).start()
+                for g in range(groups):
+                    line_copy(source, target, g).start()
 
     w_copy.wait()
     bias_copy.wait()
@@ -404,14 +408,6 @@
     extra = jnp.where(at == 0, b_hi, jnp.where(at == 1, b_mid, jnp.where(at == 2, b_lo, 0.0)))
     wcat[...] = jnp.concatenate([w_hi, w_lo, w_hi, extra.astype(BF16)], 0)
 
-    for step in range(1, n):
-        count_copy(step).wait_recv()
-    total = jnp.zeros((1, 128), I32)
-    for at in range(n):
-        prefix[at] = total
-        total = total + tally[at]
-    prefix[n] = total
-
     lane = lax.broadcasted_iota(I32, (GROUP, height), 1)
 
     def bound(index):
@@ -423,75 +419,108 @@
 
     @pl.when(flat)
     def _():
-        for g in range(groups):
-            rows_g = slice(g * GROUP, (g + 1) * GROUP)
-            for step in range(1, side):
-                seat_copy(step, g).wait_recv()
-            blocks = [turn(at, line * side + at, g) for at in range(side)]
-            for target in range(lines):
-                place = (target * side + seat) * height + lane
-                piece = jnp.where(place >= bound(line * side), blocks[0], 0.0)
-                for at in range(1, side):
-                    piece = jnp.where(place >= bound(line * side + at), blocks[at], piece)
-                pieces[target, rows_g] = jnp.where(place >= bound(line * side + side), 0.0, piece)
-                if target == 0:
-                    @pl.when(line > 0)
-                    def _(g=g):
-                        for source in range(1, lines):
-                            @pl.when(line == source)
-                            def _(source=source):
-                                down_copy(source, 0, g).start()
-        for source in range(2, lines):
-            @pl.when(line == source)
-            def _(source=source):
-                for target in range(1, source):
+        others = tally.at[pl.ds(0, n - 1)]
+        remote(others, others, count_send.at[0], count_recv.at[0], section=core).wait_recv()
+        total = jnp.zeros((1, 128), I32)
+        for at in range(n):
+            prefix[at] = total
+            total = total + tally[at]
+        prefix[n] = total
+        prefix_copy().start()
+
+        for z in range(lines):
+            @pl.when(line == z)
+            def _(z=z):
+                base = seat * height + lane
+                low, high = bound(z * side), bound(z * side + side)
+                relayed = lines > 3 and z == 3
+                for g in range(groups):
+                    at_g = slice(g * GROUP, (g + 1) * GROUP)
+                    arrived(side - 1, g, gather_recv.at[g])
+                    blocks = [turn(at, z * side + at, g) for at in range(side)]
+
+                    def choose(place):
+                        piece = jnp.where(place >= low, blocks[0], 0.0)
+                        for at in range(1, side):
+                            piece = jnp.where(place >= bound(z * side + at), blocks[at], piece)
+                        return jnp.where(place >= high, 0.0, piece)
+
+                    if relayed:
+                        place = low + ((base - low) & (side * height - 1))
+                        mixed = choose(place)
+                        pieces[2, at_g] = mixed
+                        down_copy(3, 2, g).start()
+                        joined[1, at_g] = jnp.where(place >= 3 * side * height, mixed, 0.0)
+                    else:
+                        for target in range(z):
+                            pieces[target, at_g] = choose(target * side * height + base)
+                            if not (lines > 3 and z == 2):
+                                down_copy(z, target, g).start()
+                        joined[1, at_g] = choose(z * side * height + base)
+                if lines > 3 and z == 2:
+                    top = bound(4 * side)
                     for g in range(groups):
-                        down_copy(source, target, g).start()
-
-        for g in range(groups):
-            rows_g = slice(g * GROUP, (g + 1) * GROUP)
-            joined[1, rows_g] = pieces[line, rows_g]
-            for source in range(1, lines):
-                @pl.when(line < source)
-                def _(source=source, g=g, rows_g=rows_g):
-                    down_copy(source, line, g).wait_recv()
-                    joined[1, rows_g] = joined[1, rows_g] + got[source, rows_g]
-            join_copy(g).start()
+                        at_g = slice(g * GROUP, (g + 1) * GROUP)
+                        arrived(1, g, piece_recv.at[g])
+                        for target in range(2):
+                            place = target * side * height + base
+                            inside = jnp.logical_and(place >= high, place < top)
+                            pieces[target, at_g] = jnp.where(inside, got[3, at_g], pieces[target, at_g])
+                            if target == 0:
+                                down_copy(2, 0, g).start()
+                        place = 2 * side * height + base
+                        inside = jnp.logical_and(place >= high, place < top)
+                        joined[1, at_g] = jnp.where(inside, got[3, at_g], joined[1, at_g])
+                        join_copy(g).start()
+                    for g in range(groups):
+                        down_copy(2, 1, g).start()
+                else:
+                    sources = range(z + 1, min(lines, 3))
+                    for g in range(groups):
+                        at_g = slice(g * GROUP, (g + 1) * GROUP)
+                        if sources:
+                            arrived(len(sources), g, piece_recv.at[g])
+                            block = joined[1, at_g]
+                            for source in sources:
+                                block = block + got[source, at_g]
+                            joined[1, at_g] = block
+                        join_copy(g).start()
 
     @pl.when(core == 0)
     def _():
+        prefix_copy().wait_recv()
+        for z in range(lines):
+            @pl.when(line == z)
+            def _(z=z):
+                sources = range(z, lines)
+                for g in range(groups):
+                    at_g = slice(g * GROUP, (g + 1) * GROUP)
+                    if z + 1 < lines:
+                        arrived(lines - 1 - z, g, gather_recv.at[g])
+                    blocks = [turn(at, at * side + seat, g) for at in sources]
+                    for step in [*range(1, side), 0]:
+                        place = (z * side + flip(seat, step, side)) * height + lane
+                        piece = jnp.zeros((GROUP, height), F32)
+                        for at, block in zip(sources, blocks):
+                            index = at * side + seat
+                            inside = jnp.logical_and(place >= bound(index), place < bound(index + 1))
+                            piece = jnp.where(inside, block, piece)
+                        if step:
+                            pieces[step, at_g] = piece
+                            across_copy(step, g).start()
+                        else:
+                            joined[0, at_g] = piece
         for g in range(groups):
-            rows_g = slice(g * GROUP, (g + 1) * GROUP)
-            for source in range(1, lines):
-                @pl.when(line < source)
-                def _(source=source, g=g):
-                    line_copy(source, line, g).wait_recv()
-                if source >= 2:
-                    @pl.when(line == 0)
-                    def _(source=source, g=g):
-                        relay_copy(source, g).start()
-            blocks = [turn(at, at * side + seat, g) for at in range(lines)]
-            for step in list(range(1, side)) + [0]:
-                place = (line * side + flip(seat, step, side)) * height + lane
-                piece = jnp.zeros((GROUP, height), F32)
-                for at in range(lines):
-                    index = at * side + seat
-                    inside = jnp.logical_and(place >= bound(index), place < bound(index + 1))
-                    piece = jnp.where(inside, blocks[at], piece)
-                pieces[step, rows_g] = piece
-                if step:
-                    across_copy(step, g).start()
-        for g in range(groups):
-            rows_g = slice(g * GROUP, (g + 1) * GROUP)
-            total = pieces[0, rows_g]
+            at_g = slice(g * GROUP, (g + 1) * GROUP)
+            arrived(side - 1, g, across_recv.at[g])
+            block = joined[0, at_g]
             for step in range(1, side):
-                across_copy(step, g).wait_recv()
-                total = total + got[step, rows_g]
-            joined[0, rows_g] = total
+                block = block + got[step, at_g]
+            joined[0, at_g] = block
             join_copy(g).start()
 
-    for g in range(groups):
-        join_copy(g).wait_recv()
+    other = joined.at[1 - core]
+    remote(other, other, join_send.at[0], join_recv.at[0], section=1 - core).wait_recv()
     ends = wide(prefix[n], lanes)
     for chunk in range(CHUNKS):
         at = slice(chunk * lanes, (chunk + 1) * lanes)
@@ -505,39 +534,27 @@
             lhs, wcat[...], (((0,), (0,)), ((), ())), preferred_element_type=F32
         ).astype(BF16)
 
-    for step in range(1, n):
-        count_copy(step).wait_send()
-    for g in range(groups):
-        join_copy(g).wait_send()
+    left(1, join_send.at[0])
 
     @pl.when(flat)
     def _():
-        for g in range(groups):
-            for step in range(1, side):
-                seat_copy(step, g).wait_send()
-        for source in range(1, lines):
-            @pl.when(line == source)
-            def _(source=source):
-                for target in range(source):
-                    for g in range(groups):
-                        down_copy(source, target, g).wait_send()
+        others = tally.at[pl.ds(0, n - 1)]
+        remote(others, others, count_send.at[0], count_recv.at[0], section=core).wait_send()
+        prefix_copy().wait_send()
+        left(side - 1, gather_send.at[0])
+
+    for z in range(1, lines):
+        @pl.when(jnp.logical_and(flat, line == z))
+        def _(z=z):
+            left(1 if lines > 3 and z == 3 else z, piece_send.at[0])
+
+        @pl.when(jnp.logical_and(core == 0, line == z))
+        def _(z=z):
+            left(z, gather_send.at[0])
 
     @pl.when(core == 0)
     def _():
-        for source in range(1, lines):
-            @pl.when(line == source)
-            def _(source=source):
-                for target in range(source):
-                    if target != 1:
-                        for g in range(groups):
-                            line_copy(source, target, g).wait_send()
-        for g in range(groups):
-            for source in range(2, lines):
-                @pl.when(line == 0)
-                def _(source=source, g=g):
-                    relay_copy(source, g).wait_send()
-            for step in range(1, side):
-                across_copy(step, g).wait_send()
+        left(side - 1, across_send.at[0])
 
 
 def solution(mesh):
@@ -568,14 +585,13 @@
             scratch = loads + [
                 pltpu.VMEM((n, 1, 128), I32),
                 pltpu.VMEM((n + 1, 1, 128), I32),
-                block, block, block, block,
+                block, block, block,
                 pltpu.VMEM((sections, half, height), F32),
             ] + weights + [
-                sem((4,)),
-                sem((n,)), sem((n,)),
-                sem((most, groups)), sem((most, groups)), sem((most, groups)),
-                sem((most, groups)), sem((most, groups)),
-                sem((groups,)), sem((groups,)),
+                sem((4,)), sem((2,)), sem((2,)),
+                sem((1,)), sem((groups,)),
+                sem((1,)), sem((groups,)), sem((1,)), sem((groups,)),
+                sem((1,)), sem((1,)),
             ]
         else:
             body = butterfly

time: 25.8 us -> 19.4 us (0.75)
  Pallas kernels: 24.7 us -> 18.2 us
    pallas_call x1, Pallas kernels: 24.7 us -> 18.2 us  [step(): pl.pallas_call(functools.partial(body, n), name='filter_project', out_sha...]
where the time goes in v2:
time: 19.4 us; the launch traced here: 19.2 us
  Pallas kernels  18.2 us (94%)
  local copies, waits for them, and re-layouts  0.97 us (5%)
    pallas_call x1, Pallas kernels, step(): pl.pallas_call(functools.partial(body, n), name='filter_project', out_sha...  18.2 us
    unnamed x1, local copies, waits for them, and re-layouts  0.97 us

profile of v2, /device:TPU:9, one launch (start us, length us, event | category | flops | bytes accessed | tf_op | source)
XLA Modules:
  0.0 19.2 jit_solution(2783771219042052760)
XLA Ops:
  0.0 18.2 %filter_project.1 = bf16[1024,512]{1,0:T(8,128)(2,1)S(1)} custom-call(f32[32,1024]{1,0:T(8,128)} %bitcast.3, s32[8,128]{1,0:T(8,128)} %bitcast.4, f32[64,1024]{1,0:T(8,128)} %w_hbm.1, f32[1,1024]{1,0:T(1,128)} %bitcast.5), custom_call_target="tpu_custom_call" | custom-call | tf_op jit(solution)/shard_map/filter_project/pallas_call | solution.py:613
  18.2 1.0 %copy.6 = bf16[1024,512]{1,0:T(8,128)(2,1)} copy(bf16[1024,512]{1,0:T(8,128)(2,1)S(1)} %filter_project.1) | data formatting | bytes 2097152

commit v3 on v2

--- a/solution.py
+++ b/solution.py
@@ -13,6 +13,8 @@
 LINES = 4
 GROUP = 8
 TERMS = 2
+MERGE = 2
+EARLY = 1
 F32 = jnp.float32
 BF16 = jnp.bfloat16
 I32 = jnp.int32
@@ -259,8 +261,8 @@
 def direct(
     n, table_hbm, mask_hbm, w_hbm, bias_hbm, out_ref,
     table_ref, mask_ref, bias_ref,
-    tally, prefix, gather, pieces, got, joined, w_ref, wcat,
-    load_sem, count_send, count_recv, gather_send, gather_recv,
+    tally, prefix, gather, heap, pieces, parts, got, came, joined, w_ref, wcat,
+    load_sem, count_send, count_recv, line_recv, gather_send, gather_recv, heap_recv,
     piece_send, piece_recv, across_send, across_recv, join_send, join_recv,
 ):
     half, height = table_hbm.shape
@@ -287,19 +289,27 @@
     barrier = pltpu.get_barrier_semaphore()
     pl.semaphore_signal(barrier, inc=1, device_id={"section": 1 - core})
 
+    def tells(source, target):
+        return source != target and not (source == 0 and target > 1)
+
+    def far(source, target):
+        return source > 1 and target == 0
+
     @pl.when(flat)
-    def _():
-        for step in range(1, n):
-            pl.semaphore_signal(barrier, inc=1, device_id={"rows": lax.rem(me + step, n)})
-
-    @pl.when(core == 0)
     def _():
         for step in range(1, side):
             pl.semaphore_signal(barrier, inc=1, device_id={"rows": line * side + flip(seat, step, side)})
-        for other in range(1, lines):
-            @pl.when(line < other)
-            def _(other=other):
-                pl.semaphore_signal(barrier, inc=1, device_id={"rows": other * side + seat})
+        for other in range(lines):
+            for z in range(lines):
+                if tells(other, z):
+                    @pl.when(line == z)
+                    def _(other=other):
+                        pl.semaphore_signal(barrier, inc=1, device_id={"rows": other * side + seat})
+            for z in range(other):
+                @pl.when(line == z)
+                def _(other=other, z=z):
+                    for at in range(side) if far(other, z) else [seat]:
+                        pl.semaphore_signal(barrier, inc=1, device_id={"rows": other * side + at, "section": 0})
 
     mask_copy.wait()
     mask = mask_ref[...]
@@ -317,6 +327,24 @@
     tally[me] = running
     slot = jnp.where(mask == 1, inner + jnp.concatenate(starts, 0), -1)
 
+    def far_count():
+        at = tally.at[me]
+        return [
+            pltpu.make_async_remote_copy(
+                src_ref=at, dst_ref=at, send_sem=count_send.at[1], recv_sem=count_recv.at[2],
+                device_id={"rows": to, "section": 1},
+            )
+            for to in range(side)
+        ]
+
+    for z in range(lines):
+        @pl.when(jnp.logical_and(core == 0, line == z))
+        def _(z=z):
+            pl.semaphore_wait(barrier, 1 + z + (side - 1 if z > 1 else 0))
+            if z > 1:
+                for copy in far_count():
+                    copy.start()
+
     own = jnp.where(flat, seat, line)
     table_copy.wait()
     terms = jnp.concatenate(split(table_ref[...], TERMS), 0)
@@ -339,14 +367,23 @@
     def remote(src, dst, send, recv, **to):
         return pltpu.make_async_remote_copy(src_ref=src, dst_ref=dst, send_sem=send, recv_sem=recv, device_id=to)
 
-    def blocks_of(count, g):
-        return gather.at[pl.ds(0, count), span(g)]
-
-    def count_copy(step):
-        return remote(tally.at[me], tally.at[me], count_send.at[0], count_recv.at[0], rows=lax.rem(me + step, n))
-
-    def prefix_copy():
-        return remote(prefix, prefix, count_send.at[1], count_recv.at[1], section=1 - core)
+    def seat_count():
+        at = tally.at[me]
+        return [
+            remote(at, at, count_send.at[0], count_recv.at[0], rows=line * side + flip(seat, step, side))
+            for step in range(1, side)
+        ]
+
+    def line_count(source, target):
+        low = 0 if target > source == 1 else source * side
+        at = tally.at[pl.ds(low, (source + 1) * side - low)]
+        return remote(
+            at, at, count_send.at[2 if target > source else 1], line_recv.at[source], rows=target * side + seat
+        )
+
+    def total_copy():
+        at = prefix.at[n]
+        return remote(at, at, count_send.at[3], count_recv.at[1], section=1 - core)
 
     def seat_copy(step, g):
         at = gather.at[seat, span(g)]
@@ -354,8 +391,17 @@
         return remote(at, at, gather_send.at[0], gather_recv.at[g], rows=to)
 
     def line_copy(source, target, g):
-        at = gather.at[source, span(g)]
-        return remote(at, at, gather_send.at[0], gather_recv.at[g], rows=target * side + seat)
+        return remote(
+            gather.at[source, span(g)], heap.at[source, span(g)],
+            gather_send.at[0], heap_recv.at[g], rows=target * side + seat, section=1,
+        )
+
+    def order(source):
+        every = range(groups)
+        first = [(0, g) for g in every] if source else []
+        near = [(target, g) for target in reversed(range(2, source)) for g in every]
+        after = [(source, g) for g in every] + [(1, g) for g in every if source > 1]
+        return first[:EARLY] + near + first[EARLY:] + after
 
     def down_copy(source, target, g):
         return remote(
@@ -365,39 +411,56 @@
 
     def across_copy(step, g):
         return remote(
-            pieces.at[step, span(g)], got.at[step, span(g)],
+            parts.at[step, span(g)], came.at[step, span(g)],
             across_send.at[0], across_recv.at[g], rows=line * side + flip(seat, step, side),
         )
 
-    def join_copy(g):
-        at = joined.at[core, span(g)]
+    def join_copy(which, g):
+        at = joined.at[which, span(g)]
         return remote(at, at, join_send.at[0], join_recv.at[0], section=1 - core)
 
     def arrived(count, g, sem):
-        at = blocks_of(count, g)
+        at = heap.at[pl.ds(0, count), span(g)]
         remote(at, at, sem, sem, section=core).wait_recv()
 
     def left(count, sem):
-        for at in range(0, count, side):
-            some = gather.at[pl.ds(0, min(side, count - at))]
-            remote(some, some, sem, sem, section=core).wait_send()
-
-    pl.semaphore_wait(barrier, jnp.where(flat, n, side + line))
+        at = heap.at[pl.ds(0, count)]
+        remote(at, at, sem, sem, section=core).wait_send()
+
+    def told(count, sem):
+        at = tally.at[pl.ds(0, count)]
+        remote(at, at, sem, sem, section=core).wait_recv()
+
+    def said(count, sem):
+        at = tally.at[pl.ds(0, count)]
+        remote(at, at, sem, sem, section=core).wait_send()
+
+    def extend(start, stop):
+        running = prefix[start] if start else jnp.zeros((1, 128), I32)
+        prefix[start] = running
+        for at in range(start, stop):
+            running = running + tally[at]
+            prefix[at + 1] = running
+
+    for z in range(lines):
+        ahead = sum(tells(z, other) for other in range(lines))
+        @pl.when(jnp.logical_and(flat, line == z))
+        def _(ahead=ahead):
+            pl.semaphore_wait(barrier, side + ahead)
 
     @pl.when(flat)
     def _():
-        for step in range(1, n):
-            count_copy(step).start()
+        for copy in seat_count():
+            copy.start()
         for g in range(groups):
             for step in range(1, side):
                 seat_copy(step, g).start()
 
-    for source in range(1, lines):
+    for source in range(lines):
         @pl.when(jnp.logical_and(core == 0, line == source))
         def _(source=source):
-            for target in range(source):
-                for g in range(groups):
-                    line_copy(source, target, g).start()
+            for target, g in order(source):
+                line_copy(source, target, g).start()
 
     w_copy.wait()
     bias_copy.wait()
@@ -413,114 +476,133 @@
     def bound(index):
         return wide(jnp.broadcast_to(prefix[index], (GROUP, 128)), height)
 
-    def turn(slot, index, g):
+    def turn(ref, slot, index, g):
         shift = (prefix[index] & (height - 1))[0, 0]
-        return pltpu.roll(gather[slot, g * GROUP : (g + 1) * GROUP], shift, 1)
-
-    @pl.when(flat)
-    def _():
-        others = tally.at[pl.ds(0, n - 1)]
-        remote(others, others, count_send.at[0], count_recv.at[0], section=core).wait_recv()
-        total = jnp.zeros((1, 128), I32)
-        for at in range(n):
-            prefix[at] = total
-            total = total + tally[at]
-        prefix[n] = total
-        prefix_copy().start()
-
-        for z in range(lines):
-            @pl.when(line == z)
-            def _(z=z):
-                base = seat * height + lane
-                low, high = bound(z * side), bound(z * side + side)
-                relayed = lines > 3 and z == 3
-                for g in range(groups):
-                    at_g = slice(g * GROUP, (g + 1) * GROUP)
-                    arrived(side - 1, g, gather_recv.at[g])
-                    blocks = [turn(at, z * side + at, g) for at in range(side)]
-
-                    def choose(place):
-                        piece = jnp.where(place >= low, blocks[0], 0.0)
-                        for at in range(1, side):
-                            piece = jnp.where(place >= bound(z * side + at), blocks[at], piece)
-                        return jnp.where(place >= high, 0.0, piece)
-
-                    if relayed:
-                        place = low + ((base - low) & (side * height - 1))
-                        mixed = choose(place)
-                        pieces[2, at_g] = mixed
-                        down_copy(3, 2, g).start()
-                        joined[1, at_g] = jnp.where(place >= 3 * side * height, mixed, 0.0)
+        return pltpu.roll(ref[slot, g * GROUP : (g + 1) * GROUP], shift, 1)
+
+    def routed(z):
+        base = seat * height + lane
+        told(side - 1, count_recv.at[0])
+        for target in range(z):
+            if not far(z, target):
+                line_count(z, target).start()
+        if z == 1:
+            told(side, line_recv.at[0])
+        for target in range(z + 1, lines):
+            if tells(z, target):
+                line_count(z, target).start()
+        if z > 1:
+            told(2 * side, line_recv.at[1])
+            for source in range(2, z):
+                told(side, line_recv.at[source])
+        extend(0, (z + 1) * side)
+        low, high = bound(z * side), bound(z * side + side)
+        relayed = z == 3
+        merges = z == 2 and lines > 3
+        for g in range(groups):
+            at_g = slice(g * GROUP, (g + 1) * GROUP)
+            arrived(side - 1, g, gather_recv.at[g])
+            blocks = [turn(gather, at, z * side + at, g) for at in range(side)]
+
+            def choose(place):
+                piece = jnp.where(place >= low, blocks[0], 0.0)
+                for at in range(1, side):
+                    piece = jnp.where(place >= bound(z * side + at), blocks[at], piece)
+                return jnp.where(place >= high, 0.0, piece)
+
+            if relayed:
+                mixed = choose(low + ((base - low) & (side * height - 1)))
+                pieces[2, at_g] = mixed
+                down_copy(3, 2, g).start()
+                joined[1, at_g] = jnp.where(z * side * height + base < low + side * height, mixed, 0.0)
+            else:
+                for target in range(z):
+                    pieces[target, at_g] = choose(target * side * height + base)
+                    if not merges:
+                        down_copy(z, target, g).start()
+                joined[1, at_g] = choose(z * side * height + base)
+            if relayed:
+                join_copy(1, g).start()
+        for source in range(z + 1, lines):
+            if not far(source, z):
+                told(side, line_recv.at[source])
+        if z == 0 and lines > 2:
+            told((lines - 2) * side, count_recv.at[2])
+        extend((z + 1) * side, n)
+        total_copy().start()
+        def merge():
+            for g in range(groups):
+                at_g = slice(g * GROUP, (g + 1) * GROUP)
+                arrived(1, g, piece_recv.at[g])
+                for target in range(3):
+                    place = target * side * height + base
+                    inside = jnp.logical_and(place >= high, place < high + side * height)
+                    block = jnp.where(inside, got[3, at_g], joined[1, at_g] if target == 2 else pieces[target, at_g])
+                    if target == 2:
+                        joined[1, at_g] = block
+                        join_copy(1, g).start()
                     else:
-                        for target in range(z):
-                            pieces[target, at_g] = choose(target * side * height + base)
-                            if not (lines > 3 and z == 2):
-                                down_copy(z, target, g).start()
-                        joined[1, at_g] = choose(z * side * height + base)
-                if lines > 3 and z == 2:
-                    top = bound(4 * side)
-                    for g in range(groups):
-                        at_g = slice(g * GROUP, (g + 1) * GROUP)
-                        arrived(1, g, piece_recv.at[g])
-                        for target in range(2):
-                            place = target * side * height + base
-                            inside = jnp.logical_and(place >= high, place < top)
-                            pieces[target, at_g] = jnp.where(inside, got[3, at_g], pieces[target, at_g])
-                            if target == 0:
-                                down_copy(2, 0, g).start()
-                        place = 2 * side * height + base
-                        inside = jnp.logical_and(place >= high, place < top)
-                        joined[1, at_g] = jnp.where(inside, got[3, at_g], joined[1, at_g])
-                        join_copy(g).start()
-                    for g in range(groups):
-                        down_copy(2, 1, g).start()
+                        pieces[target, at_g] = block
+                        if target == 0:
+                            down_copy(2, 0, g).start()
+            for g in range(groups):
+                down_copy(2, 1, g).start()
+
+        sources = range(z, lines)
+        for g in range(groups):
+            if merges and g == MERGE:
+                merge()
+            at_g = slice(g * GROUP, (g + 1) * GROUP)
+            arrived(lines - z, g, heap_recv.at[g])
+            turned = [turn(heap, at, at * side + seat, g) for at in sources]
+            for step in [*range(1, side), 0]:
+                place = (z * side + flip(seat, step, side)) * height + lane
+                piece = jnp.zeros((GROUP, height), F32)
+                for at, block in zip(sources, turned):
+                    index = at * side + seat
+                    inside = jnp.logical_and(place >= bound(index), place < bound(index + 1))
+                    piece = jnp.where(inside, block, piece)
+                if step:
+                    parts[step, at_g] = piece
+                    across_copy(step, g).start()
                 else:
-                    sources = range(z + 1, min(lines, 3))
-                    for g in range(groups):
-                        at_g = slice(g * GROUP, (g + 1) * GROUP)
-                        if sources:
-                            arrived(len(sources), g, piece_recv.at[g])
-                            block = joined[1, at_g]
-                            for source in sources:
-                                block = block + got[source, at_g]
-                            joined[1, at_g] = block
-                        join_copy(g).start()
-
-    @pl.when(core == 0)
-    def _():
-        prefix_copy().wait_recv()
-        for z in range(lines):
-            @pl.when(line == z)
-            def _(z=z):
-                sources = range(z, lines)
-                for g in range(groups):
-                    at_g = slice(g * GROUP, (g + 1) * GROUP)
-                    if z + 1 < lines:
-                        arrived(lines - 1 - z, g, gather_recv.at[g])
-                    blocks = [turn(at, at * side + seat, g) for at in sources]
-                    for step in [*range(1, side), 0]:
-                        place = (z * side + flip(seat, step, side)) * height + lane
-                        piece = jnp.zeros((GROUP, height), F32)
-                        for at, block in zip(sources, blocks):
-                            index = at * side + seat
-                            inside = jnp.logical_and(place >= bound(index), place < bound(index + 1))
-                            piece = jnp.where(inside, block, piece)
-                        if step:
-                            pieces[step, at_g] = piece
-                            across_copy(step, g).start()
-                        else:
-                            joined[0, at_g] = piece
-        for g in range(groups):
+                    joined[0, at_g] = piece
+        def take_flat(g):
+            froms = range(z + 1, min(lines, 3))
+            at_g = slice(g * GROUP, (g + 1) * GROUP)
+            if froms:
+                arrived(len(froms), g, piece_recv.at[g])
+                block = joined[1, at_g]
+                for source in froms:
+                    block = block + got[source, at_g]
+                joined[1, at_g] = block
+            join_copy(1, g).start()
+
+        def take_tall(g):
             at_g = slice(g * GROUP, (g + 1) * GROUP)
             arrived(side - 1, g, across_recv.at[g])
             block = joined[0, at_g]
             for step in range(1, side):
-                block = block + got[step, at_g]
+                block = block + came[step, at_g]
             joined[0, at_g] = block
-            join_copy(g).start()
-
-    other = joined.at[1 - core]
-    remote(other, other, join_send.at[0], join_recv.at[0], section=1 - core).wait_recv()
+            join_copy(0, g).start()
+
+        for g in range(groups):
+            take_tall(g)
+            if not merges and not relayed:
+                take_flat(g)
+
+    for z in range(lines):
+        @pl.when(jnp.logical_and(flat, line == z))
+        def _(z=z):
+            routed(z)
+
+    @pl.when(core == 0)
+    def _():
+        at = prefix.at[n]
+        remote(at, at, count_send.at[3], count_recv.at[1], section=1 - core).wait_recv()
+        remote(joined, joined, join_send.at[0], join_recv.at[0], section=1 - core).wait_recv()
+
     ends = wide(prefix[n], lanes)
     for chunk in range(CHUNKS):
         at = slice(chunk * lanes, (chunk + 1) * lanes)
@@ -534,27 +616,28 @@
             lhs, wcat[...], (((0,), (0,)), ((), ())), preferred_element_type=F32
         ).astype(BF16)
 
-    left(1, join_send.at[0])
-
-    @pl.when(flat)
-    def _():
-        others = tally.at[pl.ds(0, n - 1)]
-        remote(others, others, count_send.at[0], count_recv.at[0], section=core).wait_send()
-        prefix_copy().wait_send()
-        left(side - 1, gather_send.at[0])
-
-    for z in range(1, lines):
+    for z in range(lines):
         @pl.when(jnp.logical_and(flat, line == z))
         def _(z=z):
-            left(1 if lines > 3 and z == 3 else z, piece_send.at[0])
+            said(side - 1, count_send.at[0])
+            below = sum(not far(z, target) for target in range(z))
+            if below:
+                said(below * side, count_send.at[1])
+            above = sum(tells(z, target) for target in range(z + 1, lines))
+            if above:
+                said(above * side * (2 if z == 1 else 1), count_send.at[2])
+            total_copy().wait_send()
+            left(side - 1, gather_send.at[0])
+            if z:
+                left(1 if z == 3 else z, piece_send.at[0])
+            left(side - 1, across_send.at[0])
+            left(2, join_send.at[0])
 
         @pl.when(jnp.logical_and(core == 0, line == z))
         def _(z=z):
-            left(z, gather_send.at[0])
-
-    @pl.when(core == 0)
-    def _():
-        left(side - 1, across_send.at[0])
+            left(z + 1, gather_send.at[0])
+            if z > 1:
+                said(side, count_send.at[1])
 
 
 def solution(mesh):
@@ -585,11 +668,11 @@
             scratch = loads + [
                 pltpu.VMEM((n, 1, 128), I32),
                 pltpu.VMEM((n + 1, 1, 128), I32),
-                block, block, block,
+                block, block, block, block, block, block,
                 pltpu.VMEM((sections, half, height), F32),
             ] + weights + [
-                sem((4,)), sem((2,)), sem((2,)),
-                sem((1,)), sem((groups,)),
+                sem((4,)), sem((4,)), sem((3,)), sem((lines,)),
+                sem((1,)), sem((groups,)), sem((groups,)),
                 sem((1,)), sem((groups,)), sem((1,)), sem((groups,)),
                 sem((1,)), sem((1,)),
             ]

time: 19.4 us -> 18.5 us (0.954)
  the two profiles are of different devices: /device:TPU:9 before, /device:TPU:0 now
where the time goes in v3:
time: 18.5 us; the launch traced here: 18.4 us
  Pallas kernels  17.4 us (94%)
  local copies, waits for them, and re-layouts  0.97 us (5%)
    pallas_call x1, Pallas kernels, step(): pl.pallas_call(functools.partial(body, n), name='filter_project', out_sha...  17.4 us
    unnamed x1, local copies, waits for them, and re-layouts  0.97 us

profile of v3, /device:TPU:0, one launch (start us, length us, event | category | flops | bytes accessed | tf_op | source)
XLA Modules:
  0.0 18.4 jit_solution(8335198009946181604)
XLA Ops:
  0.0 17.4 %filter_project.1 = bf16[1024,512]{1,0:T(8,128)(2,1)S(1)} custom-call(f32[32,1024]{1,0:T(8,128)} %bitcast.3, s32[8,128]{1,0:T(8,128)} %bitcast.4, f32[64,1024]{1,0:T(8,128)} %w_hbm.1, f32[1,1024]{1,0:T(1,128)} %bitcast.5), custom_call_target="tpu_custom_call" | custom-call | tf_op jit(solution)/shard_map/filter_project/pallas_call | solution.py:696
  17.4 1.0 %copy.6 = bf16[1024,512]{1,0:T(8,128)(2,1)} copy(bf16[1024,512]{1,0:T(8,128)(2,1)S(1)} %filter_project.1) | data formatting | bytes 2097152

commit v4 on v3

--- a/solution.py
+++ b/solution.py
@@ -14,7 +14,7 @@
 GROUP = 8
 TERMS = 2
 MERGE = 2
-EARLY = 1
+EARLY = 4
 F32 = jnp.float32
 BF16 = jnp.bfloat16
 I32 = jnp.int32
@@ -263,7 +263,7 @@
     table_ref, mask_ref, bias_ref,
     tally, prefix, gather, heap, pieces, parts, got, came, joined, w_ref, wcat,
     load_sem, count_send, count_recv, line_recv, gather_send, gather_recv, heap_recv,
-    piece_send, piece_recv, across_send, across_recv, join_send, join_recv,
+    piece_send, piece_recv, across_send, across_recv, join_send, join_recv, ready,
 ):
     half, height = table_hbm.shape
     width = out_ref.shape[1]
@@ -292,6 +292,9 @@
     def tells(source, target):
         return source != target and not (source == 0 and target > 1)
 
+    def later(source, target):
+        return source < 2 and target > source
+
     def far(source, target):
         return source > 1 and target == 0
 
@@ -301,7 +304,7 @@
             pl.semaphore_signal(barrier, inc=1, device_id={"rows": line * side + flip(seat, step, side)})
         for other in range(lines):
             for z in range(lines):
-                if tells(other, z):
+                if tells(other, z) and not later(other, z):
                     @pl.when(line == z)
                     def _(other=other):
                         pl.semaphore_signal(barrier, inc=1, device_id={"rows": other * side + seat})
@@ -345,6 +348,30 @@
                 for copy in far_count():
                     copy.start()
 
+    def seat_count():
+        at = tally.at[me]
+        return [
+            pltpu.make_async_remote_copy(
+                src_ref=at, dst_ref=at, send_sem=count_send.at[0], recv_sem=count_recv.at[0],
+                device_id={"rows": line * side + flip(seat, step, side)},
+            )
+            for step in range(1, side)
+        ]
+
+    def enter(z):
+        ahead = sum(tells(z, other) and not later(z, other) for other in range(lines))
+        pl.semaphore_wait(barrier, side + ahead)
+        for other in range(min(z, 2)):
+            if tells(other, z):
+                pl.semaphore_signal(ready, inc=1, device_id={"rows": other * side + seat})
+        for copy in seat_count():
+            copy.start()
+
+    for z in range(min(lines, 2)):
+        @pl.when(jnp.logical_and(flat, line == z))
+        def _(z=z):
+            enter(z)
+
     own = jnp.where(flat, seat, line)
     table_copy.wait()
     terms = jnp.concatenate(split(table_ref[...], TERMS), 0)
@@ -367,13 +394,6 @@
     def remote(src, dst, send, recv, **to):
         return pltpu.make_async_remote_copy(src_ref=src, dst_ref=dst, send_sem=send, recv_sem=recv, device_id=to)
 
-    def seat_count():
-        at = tally.at[me]
-        return [
-            remote(at, at, count_send.at[0], count_recv.at[0], rows=line * side + flip(seat, step, side))
-            for step in range(1, side)
-        ]
-
     def line_count(source, target):
         low = 0 if target > source == 1 else source * side
         at = tally.at[pl.ds(low, (source + 1) * side - low)]
@@ -400,8 +420,12 @@
         every = range(groups)
         first = [(0, g) for g in every] if source else []
         near = [(target, g) for target in reversed(range(2, source)) for g in every]
-        after = [(source, g) for g in every] + [(1, g) for g in every if source > 1]
+        after = [(source, g) for g in every] + [(1, g) for g in every if source == 2]
         return first[:EARLY] + near + first[EARLY:] + after
+
+    def pass_copy(g):
+        at = heap.at[3, span(g)]
+        return remote(at, at, gather_send.at[0], heap_recv.at[g], rows=side + seat)
 
     def down_copy(source, target, g):
         return remote(
@@ -442,16 +466,13 @@
             running = running + tally[at]
             prefix[at + 1] = running
 
-    for z in range(lines):
-        ahead = sum(tells(z, other) for other in range(lines))
+    for z in range(2, lines):
         @pl.when(jnp.logical_and(flat, line == z))
-        def _(ahead=ahead):
-            pl.semaphore_wait(barrier, side + ahead)
+        def _(z=z):
+            enter(z)
 
     @pl.when(flat)
     def _():
-        for copy in seat_count():
-            copy.start()
         for g in range(groups):
             for step in range(1, side):
                 seat_copy(step, g).start()
@@ -488,9 +509,11 @@
                 line_count(z, target).start()
         if z == 1:
             told(side, line_recv.at[0])
-        for target in range(z + 1, lines):
-            if tells(z, target):
-                line_count(z, target).start()
+        above = [target for target in range(z + 1, lines) if tells(z, target)]
+        if z < 2 and above:
+            pl.semaphore_wait(ready, len(above))
+        for target in above:
+            line_count(z, target).start()
         if z > 1:
             told(2 * side, line_recv.at[1])
             for source in range(2, z):
@@ -499,6 +522,10 @@
         low, high = bound(z * side), bound(z * side + side)
         relayed = z == 3
         merges = z == 2 and lines > 3
+        if merges:
+            for g in range(groups):
+                arrived(lines - z, g, heap_recv.at[g])
+                pass_copy(g).start()
         for g in range(groups):
             at_g = slice(g * GROUP, (g + 1) * GROUP)
             arrived(side - 1, g, gather_recv.at[g])
@@ -553,7 +580,8 @@
             if merges and g == MERGE:
                 merge()
             at_g = slice(g * GROUP, (g + 1) * GROUP)
-            arrived(lines - z, g, heap_recv.at[g])
+            if not merges:
+                arrived(lines - z, g, heap_recv.at[g])
             turned = [turn(heap, at, at * side + seat, g) for at in sources]
             for step in [*range(1, side), 0]:
                 place = (z * side + flip(seat, step, side)) * height + lane
@@ -628,6 +656,8 @@
                 said(above * side * (2 if z == 1 else 1), count_send.at[2])
             total_copy().wait_send()
             left(side - 1, gather_send.at[0])
+            if z == 2 and lines > 3:
+                left(1, gather_send.at[0])
             if z:
                 left(1 if z == 3 else z, piece_send.at[0])
             left(side - 1, across_send.at[0])
@@ -635,7 +665,7 @@
 
         @pl.when(jnp.logical_and(core == 0, line == z))
         def _(z=z):
-            left(z + 1, gather_send.at[0])
+            left(min(z + 1, 3), gather_send.at[0])
             if z > 1:
                 said(side, count_send.at[1])
 
@@ -674,7 +704,7 @@
                 sem((4,)), sem((4,)), sem((3,)), sem((lines,)),
                 sem((1,)), sem((groups,)), sem((groups,)),
                 sem((1,)), sem((groups,)), sem((1,)), sem((groups,)),
-                sem((1,)), sem((1,)),
+                sem((1,)), sem((1,)), pltpu.SemaphoreType.REGULAR,
             ]
         else:
             body = butterfly

time: 18.5 us -> 17.9 us (0.968)
  Pallas kernels: 17.4 us -> 16.8 us
    pallas_call x1, Pallas kernels: 17.4 us -> 16.8 us  [step(): pl.pallas_call(functools.partial(body, n), name='filter_project', out_sha...]
where the time goes in v4:
time: 17.9 us; the launch traced here: 17.7 us
  Pallas kernels  16.8 us (94%)
  local copies, waits for them, and re-layouts  0.97 us (5%)
    pallas_call x1, Pallas kernels, step(): pl.pallas_call(functools.partial(body, n), name='filter_project', out_sha...  16.8 us
    unnamed x1, local copies, waits for them, and re-layouts  0.97 us

profile of v4, /device:TPU:0, one launch (start us, length us, event | category | flops | bytes accessed | tf_op | source)
XLA Modules:
  0.0 17.7 jit_solution(17302711323290881491)
XLA Ops:
  0.0 16.8 %filter_project.1 = bf16[1024,512]{1,0:T(8,128)(2,1)S(1)} custom-call(f32[32,1024]{1,0:T(8,128)} %bitcast.3, s32[8,128]{1,0:T(8,128)} %bitcast.4, f32[64,1024]{1,0:T(8,128)} %w_hbm.1, f32[1,1024]{1,0:T(1,128)} %bitcast.5), custom_call_target="tpu_custom_call" | custom-call | tf_op jit(solution)/shard_map/filter_project/pallas_call | solution.py:726
  16.8 1.0 %copy.6 = bf16[1024,512]{1,0:T(8,128)(2,1)} copy(bf16[1024,512]{1,0:T(8,128)(2,1)S(1)} %filter_project.1) | data formatting | bytes 2097152

commit v5 on v4

--- a/solution.py
+++ b/solution.py
@@ -13,8 +13,9 @@
 LINES = 4
 GROUP = 8
 TERMS = 2
-MERGE = 2
-EARLY = 4
+MERGE = 1
+EARLY = 3
+LIFT = 1
 F32 = jnp.float32
 BF16 = jnp.bfloat16
 I32 = jnp.int32
@@ -262,8 +263,7 @@
     n, table_hbm, mask_hbm, w_hbm, bias_hbm, out_ref,
     table_ref, mask_ref, bias_ref,
     tally, prefix, gather, heap, pieces, parts, got, came, joined, w_ref, wcat,
-    load_sem, count_send, count_recv, line_recv, gather_send, gather_recv, heap_recv,
-    piece_send, piece_recv, across_send, across_recv, join_send, join_recv, ready,
+    load_sem, send, count_recv, line_recv, gather_recv, heap_recv, piece_recv, across_recv, join_recv, ready,
 ):
     half, height = table_hbm.shape
     width = out_ref.shape[1]
@@ -334,7 +334,7 @@
         at = tally.at[me]
         return [
             pltpu.make_async_remote_copy(
-                src_ref=at, dst_ref=at, send_sem=count_send.at[1], recv_sem=count_recv.at[2],
+                src_ref=at, dst_ref=at, send_sem=send.at[0], recv_sem=count_recv.at[2],
                 device_id={"rows": to, "section": 1},
             )
             for to in range(side)
@@ -352,7 +352,7 @@
         at = tally.at[me]
         return [
             pltpu.make_async_remote_copy(
-                src_ref=at, dst_ref=at, send_sem=count_send.at[0], recv_sem=count_recv.at[0],
+                src_ref=at, dst_ref=at, send_sem=send.at[0], recv_sem=count_recv.at[0],
                 device_id={"rows": line * side + flip(seat, step, side)},
             )
             for step in range(1, side)
@@ -398,50 +398,54 @@
         low = 0 if target > source == 1 else source * side
         at = tally.at[pl.ds(low, (source + 1) * side - low)]
         return remote(
-            at, at, count_send.at[2 if target > source else 1], line_recv.at[source], rows=target * side + seat
+            at, at, send.at[0], line_recv.at[1 if target < source else 0], rows=target * side + seat
         )
 
     def total_copy():
         at = prefix.at[n]
-        return remote(at, at, count_send.at[3], count_recv.at[1], section=1 - core)
+        return remote(at, at, send.at[0], count_recv.at[1], section=1 - core)
 
     def seat_copy(step, g):
         at = gather.at[seat, span(g)]
         to = line * side + flip(seat, step, side)
-        return remote(at, at, gather_send.at[0], gather_recv.at[g], rows=to)
+        return remote(at, at, send.at[0], gather_recv.at[g], rows=to)
 
     def line_copy(source, target, g):
         return remote(
             gather.at[source, span(g)], heap.at[source, span(g)],
-            gather_send.at[0], heap_recv.at[g], rows=target * side + seat, section=1,
+            send.at[0], heap_recv.at[g], rows=target * side + seat, section=1,
         )
 
     def order(source):
         every = range(groups)
         first = [(0, g) for g in every] if source else []
         near = [(target, g) for target in reversed(range(2, source)) for g in every]
-        after = [(source, g) for g in every] + [(1, g) for g in every if source == 2]
+        after = [(source, g) for g in every] + [(1, g) for g in every if source == 2 and g >= LIFT]
         return first[:EARLY] + near + first[EARLY:] + after
+
+    def lift_copy(g):
+        at = heap.at[2, span(g)]
+        return remote(at, at, send.at[0], heap_recv.at[g], rows=side + seat)
 
     def pass_copy(g):
         at = heap.at[3, span(g)]
-        return remote(at, at, gather_send.at[0], heap_recv.at[g], rows=side + seat)
+        return remote(at, at, send.at[0], heap_recv.at[g], rows=side + seat)
 
     def down_copy(source, target, g):
         return remote(
             pieces.at[target, span(g)], got.at[source, span(g)],
-            piece_send.at[0], piece_recv.at[g], rows=target * side + seat,
+            send.at[0], piece_recv.at[g], rows=target * side + seat,
         )
 
     def across_copy(step, g):
         return remote(
             parts.at[step, span(g)], came.at[step, span(g)],
-            across_send.at[0], across_recv.at[g], rows=line * side + flip(seat, step, side),
+            send.at[0], across_recv.at[g], rows=line * side + flip(seat, step, side),
         )
 
     def join_copy(which, g):
         at = joined.at[which, span(g)]
-        return remote(at, at, join_send.at[0], join_recv.at[0], section=1 - core)
+        return remote(at, at, send.at[0], join_recv.at[0], section=1 - core)
 
     def arrived(count, g, sem):
         at = heap.at[pl.ds(0, count), span(g)]
@@ -515,9 +519,7 @@
         for target in above:
             line_count(z, target).start()
         if z > 1:
-            told(2 * side, line_recv.at[1])
-            for source in range(2, z):
-                told(side, line_recv.at[source])
+            told(z * side, line_recv.at[0])
         extend(0, (z + 1) * side)
         low, high = bound(z * side), bound(z * side + side)
         relayed = z == 3
@@ -550,9 +552,9 @@
                 joined[1, at_g] = choose(z * side * height + base)
             if relayed:
                 join_copy(1, g).start()
-        for source in range(z + 1, lines):
-            if not far(source, z):
-                told(side, line_recv.at[source])
+        above = sum(not far(source, z) for source in range(z + 1, lines))
+        if above:
+            told(above * side, line_recv.at[1])
         if z == 0 and lines > 2:
             told((lines - 2) * side, count_recv.at[2])
         extend((z + 1) * side, n)
@@ -582,6 +584,8 @@
             at_g = slice(g * GROUP, (g + 1) * GROUP)
             if not merges:
                 arrived(lines - z, g, heap_recv.at[g])
+            if z == 0 and lines > 2 and g < LIFT:
+                lift_copy(g).start()
             turned = [turn(heap, at, at * side + seat, g) for at in sources]
             for step in [*range(1, side), 0]:
                 place = (z * side + flip(seat, step, side)) * height + lane
@@ -628,8 +632,8 @@
     @pl.when(core == 0)
     def _():
         at = prefix.at[n]
-        remote(at, at, count_send.at[3], count_recv.at[1], section=1 - core).wait_recv()
-        remote(joined, joined, join_send.at[0], join_recv.at[0], section=1 - core).wait_recv()
+        remote(at, at, send.at[0], count_recv.at[1], section=1 - core).wait_recv()
+        remote(joined, joined, send.at[0], join_recv.at[0], section=1 - core).wait_recv()
 
     ends = wide(prefix[n], lanes)
     for chunk in range(CHUNKS):
@@ -647,27 +651,31 @@
     for z in range(lines):
         @pl.when(jnp.logical_and(flat, line == z))
         def _(z=z):
-            said(side - 1, count_send.at[0])
+            said(side - 1, send.at[0])
             below = sum(not far(z, target) for target in range(z))
             if below:
-                said(below * side, count_send.at[1])
+                said(below * side, send.at[0])
             above = sum(tells(z, target) for target in range(z + 1, lines))
             if above:
-                said(above * side * (2 if z == 1 else 1), count_send.at[2])
+                said(above * side * (2 if z == 1 else 1), send.at[0])
             total_copy().wait_send()
-            left(side - 1, gather_send.at[0])
+            left(side - 1, send.at[0])
             if z == 2 and lines > 3:
-                left(1, gather_send.at[0])
+                left(1, send.at[0])
             if z:
-                left(1 if z == 3 else z, piece_send.at[0])
-            left(side - 1, across_send.at[0])
-            left(2, join_send.at[0])
+                left(1 if z == 3 else z, send.at[0])
+            elif lines > 2:
+                for g in range(LIFT):
+                    lift_copy(g).wait_send()
+            left(side - 1, send.at[0])
+            left(2, send.at[0])
 
         @pl.when(jnp.logical_and(core == 0, line == z))
         def _(z=z):
-            left(min(z + 1, 3), gather_send.at[0])
+            for target, g in order(z):
+                line_copy(z, target, g).wait_send()
             if z > 1:
-                said(side, count_send.at[1])
+                said(side, send.at[0])
 
 
 def solution(mesh):
@@ -701,10 +709,9 @@
                 block, block, block, block, block, block,
                 pltpu.VMEM((sections, half, height), F32),
             ] + weights + [
-                sem((4,)), sem((4,)), sem((3,)), sem((lines,)),
-                sem((1,)), sem((groups,)), sem((groups,)),
-                sem((1,)), sem((groups,)), sem((1,)), sem((groups,)),
-                sem((1,)), sem((1,)), pltpu.SemaphoreType.REGULAR,
+                sem((4,)), sem((1,)), sem((3,)), sem((2,)),
+                sem((groups,)), sem((groups,)), sem((groups,)), sem((groups,)),
+                sem((1,)), pltpu.SemaphoreType.REGULAR,
             ]
         else:
             body = butterfly

time: 17.9 us -> 17.6 us (0.983)
  Pallas kernels: 16.8 us -> 16.5 us
    pallas_call x1, Pallas kernels: 16.8 us -> 16.5 us  [step(): pl.pallas_call(functools.partial(body, n), name='filter_project', out_sha...]
where the time goes in v5:
time: 17.6 us; the launch traced here: 17.5 us
  Pallas kernels  16.5 us (94%)
  local copies, waits for them, and re-layouts  0.97 us (6%)
    pallas_call x1, Pallas kernels, step(): pl.pallas_call(functools.partial(body, n), name='filter_project', out_sha...  16.5 us
    unnamed x1, local copies, waits for them, and re-layouts  0.97 us

profile of v5, /device:TPU:0, one launch (start us, length us, event | category | flops | bytes accessed | tf_op | source)
XLA Modules:
  0.0 17.5 jit_solution(9823893037948624916)
XLA Ops:
  0.0 16.5 %filter_project.1 = bf16[1024,512]{1,0:T(8,128)(2,1)S(1)} custom-call(f32[32,1024]{1,0:T(8,128)} %bitcast.3, s32[8,128]{1,0:T(8,128)} %bitcast.4, f32[64,1024]{1,0:T(8,128)} %w_hbm.1, f32[1,1024]{1,0:T(1,128)} %bitcast.5), custom_call_target="tpu_custom_call" | custom-call | tf_op jit(solution)/shard_map/filter_project/pallas_call | solution.py:733
  16.5 1.0 %copy.6 = bf16[1024,512]{1,0:T(8,128)(2,1)} copy(bf16[1024,512]{1,0:T(8,128)(2,1)S(1)} %filter_project.1) | data formatting | bytes 2097152

commit v6 on v5

--- a/solution.py
+++ b/solution.py
@@ -524,12 +524,11 @@
         low, high = bound(z * side), bound(z * side + side)
         relayed = z == 3
         merges = z == 2 and lines > 3
-        if merges:
-            for g in range(groups):
+        for g in range(groups):
+            at_g = slice(g * GROUP, (g + 1) * GROUP)
+            if merges:
                 arrived(lines - z, g, heap_recv.at[g])
                 pass_copy(g).start()
-        for g in range(groups):
-            at_g = slice(g * GROUP, (g + 1) * GROUP)
             arrived(side - 1, g, gather_recv.at[g])
             blocks = [turn(gather, at, z * side + at, g) for at in range(side)]
 

time: 17.6 us -> 17.6 us (level)
  no operation moved by 1% of the time
where the time goes in v6:
time: 17.6 us; the launch traced here: 17.5 us
  Pallas kernels  16.5 us (94%)
  local copies, waits for them, and re-layouts  0.97 us (6%)
    pallas_call x1, Pallas kernels, step(): pl.pallas_call(functools.partial(body, n), name='filter_project', out_sha...  16.5 us
    unnamed x1, local copies, waits for them, and re-layouts  0.97 us

profile of v6, /device:TPU:0, one launch (start us, length us, event | category | flops | bytes accessed | tf_op | source)
XLA Modules:
  0.0 17.5 jit_solution(9195540774115026112)
XLA Ops:
  0.0 16.5 %filter_project.1 = bf16[1024,512]{1,0:T(8,128)(2,1)S(1)} custom-call(f32[32,1024]{1,0:T(8,128)} %bitcast.3, s32[8,128]{1,0:T(8,128)} %bitcast.4, f32[64,1024]{1,0:T(8,128)} %w_hbm.1, f32[1,1024]{1,0:T(1,128)} %bitcast.5), custom_call_target="tpu_custom_call" | custom-call | tf_op jit(solution)/shard_map/filter_project/pallas_call | solution.py:732
  16.5 1.0 %copy.6 = bf16[1024,512]{1,0:T(8,128)(2,1)} copy(bf16[1024,512]{1,0:T(8,128)(2,1)S(1)} %filter_project.1) | data formatting | bytes 2097152
